TPU v7x, 32 devices: a whole 2x2x4 slice. The times are simulated.
32 devices in a mesh: seq: 4 (over x, core), head: 8 (over z, y).
Axes of the slice: x: 2, y: 2, z: 4, core: 2. Of those that a mesh axis runs over, the one named last changes fastest.
Arguments:
- queries: bfloat16 [256, 4096], P('seq', 'head'), may hold values from -8 to 8
- new_keys: bfloat16 [256, 256], P('seq'), may hold values from -6 to 6
- new_values: bfloat16 [256, 256], P('seq'), may hold values from -6 to 6
- cache_keys: bfloat16 [3072, 256], P('seq'), may hold values from -8 to 8
- cache_values: bfloat16 [3072, 256], P('seq'), may hold values from -6 to 6
- positions: int32 [256], replicated, may hold values from 0 to 255, each once
- cache_len: int32 [4], replicated, may hold values from 1 to 768, 1920 in all
- out_weight: bfloat16 [4096, 16384], P('head', 'seq'), may hold values from -3.5 to 3.5
Outputs:
- output: float32 [256, 16384], P(None, 'seq')
Inputs may be any that keep to these rules, and one draw needn't show every extreme that they name: A permutation of the block's positions 0 to 255. `cache_len`: entry s is the number of live slots at the start of sequence group s's 768 cache slots; later slots of that group are not attended. Some group is full.
All inputs are finite; a program needn't handle non-finite values.
Results may differ from a plain program's by a relative error of at most 0.009.
Values may be sent and summed in bfloat16 or wider, within the bound.
A program may use at most 128 MiB of HBM per device.

v0:
```python
from functools import partial
import jax
import jax.numpy as jnp
from jax import lax
from jax.sharding import PartitionSpec as P

DH = 128
GQA = 16


def key_mask(count, query_pos, positions, cache_len, stripe, tok_dev):
    index = jnp.arange(count, dtype=jnp.int32)
    span = stripe + tok_dev
    group = index // span
    offset = index % span
    groups = jnp.arange(cache_len.shape[0], dtype=jnp.int32)
    live_len = jnp.sum(jnp.where(group[:, None] == groups[None, :], cache_len[None, :], 0), axis=1)
    is_cache = offset < stripe
    token = jnp.clip(group * tok_dev + offset - stripe, 0, positions.shape[0] - 1)
    key_pos = jnp.take(positions, token)
    return jnp.where(
        is_cache[None, :], (offset < live_len)[None, :], key_pos[None, :] <= query_pos[:, None]
    )


def softmax_step(
    state, block, begin, query_heads, query_pos, positions, cache_len, stripe, tok_dev
):
    running_max, running_sum, weighted = state
    keys = block[:, :DH]
    values = block[:, DH:]
    scores = jnp.einsum(
        "thd,kd->thk", query_heads, keys, preferred_element_type=jnp.float32
    ) * DH ** (-0.5)
    shown = key_mask(block.shape[0], query_pos, positions, cache_len, stripe, tok_dev)[:, None, :]
    scores = jnp.where(shown, scores, -1e30)
    new_max = jnp.maximum(running_max, jnp.max(scores, axis=2))
    expo = jnp.where(shown, jnp.exp(scores - new_max[:, :, None]), 0.0)
    running_sum = jnp.sum(expo, axis=2)
    weighted = jnp.einsum(
        "thk,kd->thd", expo.astype(jnp.bfloat16), values, preferred_element_type=jnp.float32
    )
    return (new_max, running_sum, weighted)


def empty_state(rows, heads_dev):
    return (
        jnp.full((rows, heads_dev), -1e30, jnp.float32),
        jnp.zeros((rows, heads_dev), jnp.float32),
        jnp.zeros((rows, heads_dev, DH), jnp.float32),
    )


def body(queries, new_keys, new_values, cache_keys, cache_values, positions, cache_len, out_weight):
    tok_dev = queries.shape[0]
    heads_dev = queries.shape[1] // DH
    stripe = cache_keys.shape[0]
    seq_index = lax.axis_index("seq")
    head_index = lax.axis_index("head")
    column = head_index * heads_dev // GQA * DH
    own_keys = jnp.concatenate(
        [
            lax.dynamic_slice_in_dim(cache_keys, column, DH, 1),
            lax.dynamic_slice_in_dim(new_keys, column, DH, 1),
        ],
        axis=0,
    )
    own_values = jnp.concatenate(
        [
            lax.dynamic_slice_in_dim(cache_values, column, DH, 1),
            lax.dynamic_slice_in_dim(new_values, column, DH, 1),
        ],
        axis=0,
    )
    key_block = jnp.concatenate([own_keys, own_values], axis=1)
    query_heads = queries.reshape(tok_dev, heads_dev, DH)
    query_pos = lax.dynamic_slice_in_dim(positions, seq_index * tok_dev, tok_dev)
    stepper = partial(
        softmax_step,
        query_heads=query_heads,
        query_pos=query_pos,
        positions=positions,
        cache_len=cache_len,
        stripe=stripe,
        tok_dev=tok_dev,
    )
    final_max, final_sum, weighted = stepper(
        empty_state(tok_dev, heads_dev),
        lax.all_gather(key_block, "seq", axis=0, tiled=True),
        jnp.int32(0),
    )
    attended = (
        (weighted / final_sum[:, :, None]).astype(jnp.bfloat16).reshape(tok_dev, heads_dev * DH)
    )
    partial_out = jnp.dot(
        lax.all_gather(attended, "seq", axis=0, tiled=True),
        out_weight,
        preferred_element_type=jnp.float32,
    )
    return lax.psum(partial_out, "head")


def solution(mesh):
    placed = (
        P("seq", "head"),
        P("seq", None),
        P("seq", None),
        P("seq", None),
        P("seq", None),
        P(),
        P(),
        P("head", "seq"),
    )
    return jax.shard_map(
        body, mesh=mesh, in_specs=placed, out_specs=P(None, "seq"), check_vma=False
    )
```

profile of v0, /device:TPU:0, one launch (start us, length us, event | category | flops | bytes accessed | tf_op | source)
XLA Modules:
  0.0 214.3 jit_solution(2551049296829856070)
XLA Ops:
  6.5 0.0 copy-start
  6.5 0.0 copy-start.1
  6.5 0.0 all-gather.2.cloned.1.call-start
  6.5 0.8 constant_dynamic-slice_fusion
  7.3 1.0 constant_dynamic-slice_fusion.1
  8.4 0.8 maximum_maximum_fusion
  9.2 0.0 all-gather.2.cloned.1.call-update
  9.2 0.0 all-reduce.2.cloned.1.call-start
  9.3 0.8 dynamic_slice.15
  10.0 0.1 fusion.28
  10.1 0.0 copy-done.1
  10.2 0.0 copy-start.3
  10.2 19.9 %gather_fusion = s32[3328]{0:T(1024)S(1)} fusion(s32[256]{0:T(256)S(1)} %copy-done.1, s32[4096]{0:T(1024)S(1)} %pad_clamp_fusion), kind=kCustom, calls=%fused_computation | custom fusion | bytes 39936 | tf_op jit(solution)/shard_map/jit(_take)/gather | solution.py:20
  30.1 0.0 copy-done.3
  30.1 0.1 select_reduce_fusion
  30.3 0.2 compare_select_fusion
  30.5 2.0 all-gather.2.cloned.1.call-done
  32.4 0.0 copy-done
  32.4 0.0 copy-start.4
  32.5 2.2 %fusion.33 = (f32[64,4]{0,1:T(4,128)S(1)}, f32[64,4,3328]{2,0,1:T(8,128)S(1)}) fusion(bf16[3328,256]{1,0:T(8,128)(2,1)} %all-gather.2.cloned.1.call-done, pred[64,3328]{1,0:T(8,128)(4,1)S(1)} %compare_select_fusion, bf16[64,512]{1,0:T(8,128)(2,1)S(1)} %copy-done), kind=kOutput, calls=%fused_computation.55 | convolution fusion | flops 220659456 | bytes 4539392 | tf_op jit(solution)/shard_map/thd,kd->thk/dot_general | solution.py:32
  34.6 0.8 fusion.2
  35.5 0.0 copy-done.4
  35.5 0.0 copy-start.2
  35.5 0.8 fusion.15
  36.3 5.9 %all_gather.7 = bf16[256,512]{1,0:T(8,128)(2,1)S(1)} all-gather(bf16[64,512]{1,0:T(8,128)(2,1)S(1)} %bitcast.28), channel_id=1, replica_groups=mesh['seq'=4,'head'=8] {'seq'}, dimensions={0}, use_global_device_ids=true | all-gather | bytes 327680 | tf_op jit(solution)/shard_map/all_gather | solution.py:96
  42.2 0.0 copy-done.2
  42.2 3.3 %fusion.34 = f32[256,4096]{1,0:T(8,128)} fusion(bf16[256,512]{1,0:T(8,128)(2,1)S(1)} %all_gather.7, bf16[512,4096]{1,0:T(8,128)(2,1)S(1)} %copy-done.2), kind=kOutput, calls=%fused_computation.56 | convolution fusion | flops 1073741824 | bytes 8650752 | tf_op jit(solution)/shard_map/dot_general | solution.py:95
  45.5 0.0 all-reduce.2.cloned.1.call-update
  45.5 157.3 %all-reduce.2.cloned.1.call-done = f32[256,4096]{1,0:T(8,128)} async-done(((f32[256,4096]{1,0:T(8,128)}), f32[256,4096]{1,0:T(8,128)}) %all-reduce.2.cloned.1.call-update) | async-done | bytes 4194320 | tf_op jit(solution)/shard_map/psum | solution.py:100
  202.8 4.7 %copy.25 = f32[256,4096]{1,0:T(8,128)} copy(f32[256,4096]{1,0:T(8,128)} %all-reduce.2.cloned.1.call-done) | data formatting | bytes 8388608
  (6 shorter events, 0.1 us)
Async XLA Ops:
  6.5 25.9 %copy-start = (bf16[64,512]{1,0:T(8,128)(2,1)S(1)}, bf16[64,512]{1,0:T(8,128)(2,1)}, u32[]{:S(2)}) copy-start(bf16[64,512]{1,0:T(8,128)(2,1)} %param.8) | copy-start | bytes 196612
  6.5 3.6 %copy-start.1 = (s32[256]{0:T(256)S(1)}, s32[256]{0:T(256)}, u32[]{:S(2)}) copy-start(s32[256]{0:T(256)} %param.13) | copy-start | bytes 3076
  6.5 25.9 %all-gather.2.cloned.1.call-start = ((), (), s32[]{:S(2)}) async-start(), calls=%async_computation | async-start | bytes 2129920 | tf_op jit(solution)/shard_map/all_gather | solution.py:89
  9.2 193.6 %all-reduce.2.cloned.1.call-start = ((), (), s32[]{:S(2)}) async-start(), calls=%async_computation.1 | async-start | bytes 8388608 | tf_op jit(solution)/shard_map/psum | solution.py:100
  10.2 19.9 %copy-start.3 = (s32[4]{0:T(128)S(1)}, s32[4]{0:T(128)}, u32[]{:S(2)}) copy-start(s32[4]{0:T(128)} %param.14) | copy-start | bytes 52
  32.4 3.0 %copy-start.4 = (bf16[3328,256]{1,0:T(8,128)(2,1)S(1)}, bf16[3328,256]{1,0:T(8,128)(2,1)}, u32[]{:S(2)}) copy-start(bf16[3328,256]{1,0:T(8,128)(2,1)} %all-gather.2.cloned.1.call-done) | copy-start | bytes 5111812
  35.5 6.8 %copy-start.2 = (bf16[512,4096]{1,0:T(8,128)(2,1)S(1)}, bf16[512,4096]{1,0:T(8,128)(2,1)}, u32[]{:S(2)}) copy-start(bf16[512,4096]{1,0:T(8,128)(2,1)} %param.15) | copy-start | bytes 12582916
Sparse Core Ops, SparseCore 0:
  9.3 23.0 all-gather.1
  45.7 157.1 all-reduce.1
where the time goes:
time: 215 us; the launch traced here: 214 us
  waiting for transfers between devices  159 us (74%)
  local copies, waits for them, and re-layouts  27.2 us (13%)
  between operations  13.5 us (6%)
  matrix products  6.27 us (3%)
  blocking collectives  5.91 us (3%)
  other arithmetic  2.15 us (1%)
    psum x1, waiting for transfers between devices, body(): return lax.psum(partial_out, 'head')  157 us
    gather x1, local copies, waits for them, and re-layouts, key_mask(): key_pos = jnp.take(positions, token)  19.9 us
    all_gather x1, blocking collectives, body(): lax.all_gather(attended, 'seq', axis=0, tiled=True)  5.91 us
    unnamed x11, local copies, waits for them, and re-layouts  4.67 us
  transfers between devices with their start and end apart: 2, of which 2 were waited for; matrix products, arithmetic and copies ran while one was open for 10% of the time, Pallas kernels for 0%

commit v1 on v0

--- a/solution.py
+++ b/solution.py
@@ -6,6 +6,11 @@
 
 DH = 128
 GQA = 16
+
+
+def summed_here(x, name):
+    shards = lax.all_gather(x, name)
+    return jnp.sum(shards, axis=0)
 
 
 def key_mask(count, query_pos, positions, cache_len, stripe, tok_dev):
@@ -97,7 +102,7 @@
         out_weight,
         preferred_element_type=jnp.float32,
     )
-    return lax.psum(partial_out, "head")
+    return summed_here(partial_out, "head")
 
 
 def solution(mesh):

time: 215 us -> 705 us (3.28)
  waiting for transfers between devices: 159 us -> 641 us
  other arithmetic: 2.15 us -> 16.2 us
    all_gather x0 -> x1, waiting for transfers between devices: none -> 639 us  [summed_here(): shards = lax.all_gather(x, name)]
    psum x1 -> x0, waiting for transfers between devices: 157 us -> none  [body(): return lax.psum(partial_out, 'head')]
    reduce_sum x0 -> x1, other arithmetic: none -> 14 us  [summed_here(): return jnp.sum(shards, axis=0)]
  transfers between devices with their start and end apart: 2 -> 2, of which waited for: 2 -> 2; matrix products, arithmetic and copies ran while one was open for 10% -> 3% of each run, Pallas kernels for 0% -> 0%
where the time goes in v1:
time: 705 us
  waiting for transfers between devices  641 us (91%)
  local copies, waits for them, and re-layouts  22.5 us (3%)
  other arithmetic  16.2 us (2%)
  between operations  13.5 us (2%)
    all_gather x1, waiting for transfers between devices, summed_here(): shards = lax.all_gather(x, name)  639 us
    gather x1, local copies, waits for them, and re-layouts, key_mask(): key_pos = jnp.take(positions, token)  19.9 us
  transfers between devices with their start and end apart: 2, of which 2 were waited for; matrix products, arithmetic and copies ran while one was open for 3% of the time, Pallas kernels for 0%

profile of v1, /device:TPU:0, one launch (start us, length us, event | category | flops | bytes accessed | tf_op | source)
XLA Modules:
  0.0 705.0 jit_solution(14442013560388513237)
XLA Ops:
  6.5 0.0 copy-start
  6.5 0.0 copy-start.1
  6.5 0.0 all-gather.4.cloned.1.call-start
  6.5 0.8 constant_dynamic-slice_fusion
  7.3 1.0 constant_dynamic-slice_fusion.1
  8.4 0.8 maximum_maximum_fusion
  9.2 0.0 all-gather.4.cloned.1.call-update
  9.2 0.0 all-gather.6.cloned.1.call-start
  9.3 0.8 dynamic_slice.15
  10.0 0.1 fusion.28
  10.1 0.0 copy-done.1
  10.2 0.0 copy-start.3
  10.2 19.9 %gather_fusion = s32[3328]{0:T(1024)S(1)} fusion(s32[256]{0:T(256)S(1)} %copy-done.1, s32[4096]{0:T(1024)S(1)} %pad_clamp_fusion), kind=kCustom, calls=%fused_computation | custom fusion | bytes 39936 | tf_op jit(solution)/shard_map/jit(_take)/gather | solution.py:25
  30.1 0.0 copy-done.3
  30.1 0.1 select_reduce_fusion
  30.3 0.2 compare_select_fusion
  30.5 2.0 all-gather.4.cloned.1.call-done
  32.4 0.0 copy-done
  32.4 0.0 copy-start.4
  32.5 2.2 fusion.33
  34.6 0.8 fusion.2
  35.5 0.0 copy-done.4
  35.5 0.0 copy-start.2
  35.5 0.8 fusion.15
  36.3 5.9 all_gather.13
  42.2 0.0 copy-done.2
  42.2 3.3 fusion.34
  45.5 0.0 all-gather.6.cloned.1.call-update
  45.5 638.6 %all-gather.6.cloned.1.call-done = f32[2048,4096]{1,0:T(8,128)} async-done(((f32[256,4096]{1,0:T(8,128)}), f32[2048,4096]{1,0:T(8,128)}) %all-gather.6.cloned.1.call-update) | async-done | bytes 33554448 | tf_op jit(solution)/shard_map/all_gather | solution.py:12
  684.1 14.0 %reduce_sum.29 = f32[256,4096]{1,0:T(8,128)} reduce(f32[8,256,4096]{2,1,0:T(8,128)} %bitcast.29, f32[]{:T(128)} %constant.77.clone.1), dimensions={0}, to_apply=%region_3.4 | reduce | flops 7340032 | bytes 37748740 | tf_op jit(solution)/shard_map/reduce_sum | solution.py:13
  (6 shorter events, 0.1 us)
Async XLA Ops:
  6.5 25.9 %copy-start = (bf16[64,512]{1,0:T(8,128)(2,1)S(1)}, bf16[64,512]{1,0:T(8,128)(2,1)}, u32[]{:S(2)}) copy-start(bf16[64,512]{1,0:T(8,128)(2,1)} %param.8) | copy-start | bytes 196612
  6.5 3.6 copy-start.1
  6.5 25.9 %all-gather.4.cloned.1.call-start = ((), (), s32[]{:S(2)}) async-start(), calls=%async_computation | async-start | bytes 2129920 | tf_op jit(solution)/shard_map/all_gather | solution.py:94
  9.2 674.9 %all-gather.6.cloned.1.call-start = ((), (), s32[]{:S(2)}) async-start(), calls=%async_computation.1 | async-start | bytes 37748736 | tf_op jit(solution)/shard_map/all_gather | solution.py:12
  10.2 19.9 %copy-start.3 = (s32[4]{0:T(128)S(1)}, s32[4]{0:T(128)}, u32[]{:S(2)}) copy-start(s32[4]{0:T(128)} %param.14) | copy-start | bytes 52
  32.4 3.0 copy-start.4
  35.5 6.8 copy-start.2
Sparse Core Ops, SparseCore 0:
  9.3 23.0 all-gather.3
  45.7 638.4 all-gather.5
